TPU v7x, 32 devices: a whole 2x2x4 slice. The times are simulated.
32 devices in a mesh: tau: 4 (over x, core), tile: 8 (over z, y).
Axes of the slice: x: 2, y: 2, z: 4, core: 2. Of those that a mesh axis runs over, the one named last changes fastest.
Arguments:
- occupied: bfloat16 [4, 1024, 128, 128], P('tau', 'tile'), may hold values from -6 to 6
- virtual: bfloat16 [4, 1024, 128, 128], P('tau', 'tile'), may hold values from -0.125 to 0.125
- cos_weights: float32 [4, 4], replicated, may hold values from -1 to 1
- pair_occ: int32 [1536, 16], P('tile'), may hold values from 0 to 127
- pair_virt: int32 [1536, 16], P('tile'), may hold values from 0 to 127
- partial_target_tile: int32 [1536], P('tile'), may hold values from 0 to 255, as said below
Outputs:
- spectrum: float32 [4, 256, 128, 128], P(None, 'tile', 'tau')
Inputs may be any that keep to these rules, and one draw needn't show every extreme that they name: `partial_target_tile`: within each aligned block of 192 entries, no owner (values d * 32 to (d + 1) * 32 - 1 for owner d) is named more than 48 times; one owner is named exactly 48 times in every block.
All inputs are finite; a program needn't handle non-finite values.
Results may differ from a plain program's by a relative error of at most 0.0003.
Values sent between devices are 32-bit elements; how exact they have to be, the bound alone decides.
A program may use at most 192 MiB of HBM per device.

v0:
```python
import functools
import math

import jax
import jax.numpy as jnp
from jax import lax
from jax.experimental import pallas as pl
from jax.experimental.pallas import tpu as pltpu
from jax.sharding import PartitionSpec as P

CHI_DEV = 32
UNIT = 2
Z_FIRST = 3 / 16
BUDGET = 46 * 1024 * 1024
MESH = pl.DeviceIdType.MESH


def products_kernel(first, terms, chi_dev, occ_idx, virt_idx, target, occ, virt, out):
    owners, units, groups, each, rows, width = out.shape
    span = units * each
    count = target.shape[0]

    @pl.loop(0, owners)
    def _(d):
        out[d] = jnp.zeros(out.shape[1:], out.dtype)

    unroll = math.gcd(count, 4) if span == chi_dev else 1

    @pl.loop(0, count, unroll=unroll)
    def _(p):
        tile = target[p]
        owner = tile // chi_dev
        place = tile - owner * chi_dev - first

        def add():
            unit = place // each
            left = [occ[occ_idx[j, p]] for j in range(terms)]
            right = [virt[virt_idx[j, p]] for j in range(terms)]
            acc = jnp.dot(
                jnp.concatenate(left, axis=1),
                jnp.concatenate(right, axis=0),
                preferred_element_type=jnp.float32,
            )
            for g in range(groups):
                out[owner, unit, g, place - unit * each] += acc[g * rows : (g + 1) * rows]

        if span == chi_dev:
            add()
        else:
            pl.when((place >= 0) & (place < span))(add)


def products(occ, virt, occ_idx, virt_idx, target, first, span, each, owners, groups):
    terms = occ_idx.shape[1]
    size = occ.shape[1]
    smem = pl.BlockSpec(memory_space=pltpu.SMEM)
    vmem = pl.BlockSpec(memory_space=pltpu.VMEM)
    return pl.pallas_call(
        functools.partial(products_kernel, first, terms, CHI_DEV),
        out_shape=jax.ShapeDtypeStruct(
            (owners, span // each, groups, each, size // groups, size), jnp.float32
        ),
        in_specs=[smem, smem, smem, vmem, vmem],
        out_specs=vmem,
        compiler_params=pltpu.CompilerParams(vmem_limit_bytes=56 * 1024 * 1024),
        cost_estimate=pl.CostEstimate(
            flops=2 * target.shape[0] * terms * size**3 * span // CHI_DEV,
            bytes_accessed=occ.size * 4 + owners * span * size * size * 4,
            transcendentals=0,
        ),
    )(occ_idx.T, virt_idx.T, target, occ, virt)


def line_slots(n):
    if n == 1:
        return 0
    return 1 if n == 2 else 2 * (n - 1)


class Line:
    def __init__(self, n, place, device, own, slots, send_sem, recv_sem, hold=None):
        self.hold = hold
        self.n, self.place, self.device = n, place, device
        self.own, self.slots, self.send_sem, self.recv_sem = own, slots, send_sem, recv_sem

    def slot(self, right, d):
        if right:
            return d - 1
        return d if self.n == 2 else self.n - 1 + d

    def copy(self, right, u, d, src, back=False):
        s = self.slot(right, d)
        k = u * line_slots(self.n) + s
        return pltpu.make_async_remote_copy(
            src_ref=src,
            dst_ref=self.slots.at[s, u],
            send_sem=self.send_sem.at[k],
            recv_sem=self.recv_sem.at[k],
            device_id={"tile": self.device(1 if right != back else -1)},
            device_id_type=MESH,
        )

    def routes(self):
        for right in (True, False):
            for d in range(self.n - 1, 0, -1) if right else range(self.n - 1):
                yield right, d

    def launch(self, u):
        for right, d in self.routes():
            @pl.when(self.place == (0 if right else self.n - 1))
            def _():
                self.copy(right, u, d, self.own(d, u)).start()

    def merge(self, u):
        if self.n == 2:
            return
        for right, d in self.routes():
            inner = (self.place > 0) & (self.place < d) if right else (
                (self.place < self.n - 1) & (self.place > d))

            @pl.when(inner)
            def _():
                here = self.slots.at[self.slot(right, d), u]
                copy = self.copy(right, u, d, here)
                copy.wait_recv()
                own = self.own(d, u)
                if self.hold is not None:
                    buffer, sem = self.hold
                    fetch = pltpu.make_async_copy(own, buffer, sem)
                    fetch.start()
                    fetch.wait()
                    own = buffer
                here[...] += own[...]
                copy.start()

    def final(self, u, into):
        for right in (True, False):
            @pl.when(self.place > 0 if right else self.place < self.n - 1)
            def _():
                k = self.slot(right, self.place)
                here = self.slots.at[k, u]
                self.copy(right, u, self.place, here, back=True).wait_recv()
                into[...] += here[...]

    def drain(self, u):
        for right, d in self.routes():
            @pl.when(self.place < d if right else self.place > d)
            def _():
                self.copy(right, u, d, self.slots.at[self.slot(right, d), u]).wait_send()


def scatter_kernel(ny, nz, groups, weights, dense, out, mine, y_slots, z_slots, times,
                   load_sem, y_send, y_recv, z_send, z_recv, t_send, t_recv, hold, hold_sem,
                   both, z2_slots, y2_slots, both_sem, z2_send, z2_recv, y2_send, y2_recv):
    tau = lax.axis_index("tau")
    tile = lax.axis_index("tile")
    z, y = tile // ny, tile % ny
    units = mine.shape[0]
    lead = both.shape[0]
    last = units - lead
    each = mine.shape[3]
    freqs = out.shape[0]

    y_line = Line(ny, y, lambda step: tile + step, lambda d, u: dense.at[:, d, u],
                  y_slots, y_send, y_recv, (hold, hold_sem))
    z_line = Line(nz, z, lambda step: tile + step * ny, lambda d, u: mine.at[u, d],
                  z_slots, z_send, z_recv)

    z2_line = Line(nz, z, z_line.device, lambda d, u: both.at[u, d], z2_slots, z2_send, z2_recv)
    y2_line = Line(ny, y, y_line.device, lambda d, u: both.at[u, z, d], y2_slots, y2_send, y2_recv)

    barrier = pltpu.get_barrier_semaphore()
    for step in range(1, groups):
        pl.semaphore_signal(barrier, inc=1, device_id={"tau": (tau + step) % groups},
                            device_id_type=MESH)
    for step in range(1, ny):
        pl.semaphore_signal(barrier, inc=1, device_id={"tile": z * ny + (y + step) % ny},
                            device_id_type=MESH)
    for step in range(1, nz):
        pl.semaphore_signal(barrier, inc=1, device_id={"tile": (z + step) % nz * ny + y},
                            device_id_type=MESH)
    pl.semaphore_wait(barrier, groups - 1 + ny - 1 + nz - 1)

    def load(u):
        return pltpu.make_async_copy(dense.at[:, y, u], mine.at[u], load_sem.at[u])

    def swap(u, step):
        other = (tau + step) % groups
        return pltpu.make_async_remote_copy(
            src_ref=mine.at[u, z, other],
            dst_ref=times.at[u, tau],
            send_sem=t_send.at[u * groups + step],
            recv_sem=t_recv.at[u * groups + tau],
            device_id={"tau": other},
            device_id_type=MESH,
        )

    def arrived(u, source):
        return pltpu.make_async_remote_copy(
            src_ref=mine.at[u, z, 0],
            dst_ref=times.at[u, source],
            send_sem=t_send.at[u * groups],
            recv_sem=t_recv.at[u * groups + source],
            device_id={"tau": source},
            device_id_type=MESH,
        )

    def whole(w):
        return pltpu.make_async_copy(dense.at[:, :, last + w], both.at[w], both_sem.at[w])

    @pl.loop(0, lead)
    def _(w):
        whole(w).start()

    @pl.loop(0, last)
    def _(u):
        y_line.launch(u)
        load(u).start()

    @pl.loop(0, lead)
    def _(w):
        whole(w).wait()
        z2_line.launch(w)

    @pl.loop(0, lead)
    def _(w):
        z2_line.merge(w)

    @pl.loop(0, units + 2)
    def _(t):
        @pl.when(t < last)
        def _():
            load(t).wait()
            y_line.merge(t)
            y_line.final(t, mine.at[t])
            z_line.launch(t)

        @pl.when(t < lead)
        def _():
            z2_line.final(t, both.at[t, z])
            y2_line.launch(t)

        @pl.when((t >= 1) & (t < last + 1))
        def _():
            u = t - 1
            z_line.merge(u)
            z_line.final(u, mine.at[u, z])

        @pl.when((t >= last + 1) & (t < units + 1))
        def _():
            w = t - 1 - last
            y2_line.merge(w)
            mine[t - 1, z] = both[w, z, y]
            y2_line.final(w, mine.at[t - 1, z])

        @pl.when((t >= 1) & (t < units + 1))
        def _():
            u = t - 1
            for step in range(1, groups):
                swap(u, step).start()
            times[u, tau] = mine[u, z, tau]

        @pl.when(t >= 2)
        def _():
            u = t - 2
            for step in range(1, groups):
                arrived(u, (tau + step) % groups).wait_recv()
            for e in range(each):
                for k in range(freqs):
                    total = weights[k, 0] * times[u, 0, e]
                    for s in range(1, groups):
                        total += weights[k, s] * times[u, s, e]
                    out[k, u * each + e] = total

    @pl.loop(0, lead)
    def _(w):
        z2_line.drain(w)
        y2_line.drain(w)

    @pl.loop(0, last)
    def _(u):
        y_line.drain(u)
        z_line.drain(u)

    @pl.loop(0, units)
    def _(u):
        for step in range(1, groups):
            swap(u, step).wait_send()


def scatter(dense, weights, ny, nz, groups):
    owners, units, _, each, rows, width = dense.shape
    freqs = weights.shape[0]
    block = (groups, each, rows, width)
    lead = max(1, int(units * Z_FIRST))
    ys, zs = max(line_slots(ny), 1), max(line_slots(nz), 1)
    dma = pltpu.SemaphoreType.DMA
    return pl.pallas_call(
        functools.partial(scatter_kernel, ny, nz, groups),
        out_shape=jax.ShapeDtypeStruct((freqs, units * each, rows, width), jnp.float32),
        in_specs=[pl.BlockSpec(memory_space=pltpu.SMEM), pl.BlockSpec(memory_space=pl.ANY)],
        out_specs=pl.BlockSpec(memory_space=pltpu.VMEM),
        scratch_shapes=[
            pltpu.VMEM((units, nz) + block, jnp.float32),
            pltpu.VMEM((ys, units, nz) + block, jnp.float32),
            pltpu.VMEM((zs, units) + block, jnp.float32),
            pltpu.VMEM((units, groups, each, rows, width), jnp.float32),
            dma((units,)),
            dma((units * ys,)),
            dma((units * ys,)),
            dma((units * zs,)),
            dma((units * zs,)),
            dma((units * groups,)),
            dma((units * groups,)),
            pltpu.VMEM((nz,) + block if ny > 2 else (8, 128), jnp.float32),
            dma,
            pltpu.VMEM((lead, nz, ny) + block, jnp.float32),
            pltpu.VMEM((zs, lead, ny) + block, jnp.float32),
            pltpu.VMEM((ys, lead) + block, jnp.float32),
            dma((lead,)),
            dma((lead * zs,)),
            dma((lead * zs,)),
            dma((lead * ys,)),
            dma((lead * ys,)),
        ],
        compiler_params=pltpu.CompilerParams(
            collective_id=0, has_side_effects=True, vmem_limit_bytes=58 * 1024 * 1024),
    )(weights, dense.reshape((nz, ny) + dense.shape[1:]))


def body(occupied, virtual, cos_weights, pair_occ, pair_virt, partial_target_tile):
    owners = lax.axis_size("tile")
    groups = lax.axis_size("tau")
    size = occupied.shape[2]
    ny = 1
    while 2 * ny * 2 * ny <= owners:
        ny *= 2
    nz = owners // ny
    tile_bytes = 4 * size * size
    span = CHI_DEV
    while span > UNIT and span * tile_bytes * (
        nz * (1 + line_slots(ny)) + line_slots(nz) + 2
    ) > BUDGET:
        span //= 2
    results = []
    for q in range(CHI_DEV // span):
        dense = products(
            occupied[0], virtual[0], pair_occ, pair_virt, partial_target_tile,
            q * span, span, min(UNIT, span), owners, groups,
        )
        results.append(scatter(dense, cos_weights, ny, nz, groups))
    return results[0] if len(results) == 1 else jnp.concatenate(results, axis=1)


def solution(mesh):
    in_specs = (
        P("tau", "tile", None, None),
        P("tau", "tile", None, None),
        P(),
        P("tile", None),
        P("tile", None),
        P("tile"),
    )
    out_specs = P(None, "tile", "tau", None)
    return jax.shard_map(body, mesh=mesh, in_specs=in_specs, out_specs=out_specs, check_vma=False)
```

profile of v0, /device:TPU:9, one launch (start us, length us, event | category | flops | bytes accessed | tf_op | source)
XLA Modules:
  0.0 253.7 jit_solution(5460998020692210545)
XLA Ops:
  0.0 44.2 %shard_map.64 = f32[8,16,4,2,32,128]{5,4,3,2,1,0:T(8,128)} custom-call(s32[16,192]{1,0:T(8,128)} %bitcast.8, s32[16,192]{1,0:T(8,128)} %bitcast.9, s32[192]{0:T(256)} %target.1, bf16[128,128,128]{2,1,0:T(8,128)(2,1)} %bitcast.6, bf16[128,128,128]{2,1,0:T(8,128)(2,1)} %bitcast.7), custom_call_target="tpu_custom_call" | custom-call | flops 12884901888 | bytes 25165824 | tf_op jit(solution)/shard_map/pallas_call | solution.py:58
  44.2 206.3 %shard_map.65 = f32[4,32,32,128]{3,2,1,0:T(8,128)} custom-call(f32[4,4]{1,0:T(4,128)} %weights.1, f32[4,2,16,4,2,32,128]{6,5,4,3,2,1,0:T(8,128)} %bitcast.5), custom_call_target="tpu_custom_call" | custom-call | tf_op jit(solution)/shard_map/pallas_call | solution.py:298
  250.6 3.1 %copy.8 = f32[4,32,32,128]{3,2,1,0:T(8,128)} copy(f32[4,32,32,128]{3,2,1,0:T(8,128)} %shard_map.65) | data formatting | bytes 4194304
where the time goes:
time: 258 us; the launch traced here: 254 us
  Pallas kernels  251 us (97%)
  local copies, waits for them, and re-layouts  3.08 us (1%)
    pallas_call x1, Pallas kernels, scatter(): pl.pallas_call(functools.partial(scatter_kernel, ny, nz, groups), out_sha...  206 us
    pallas_call x1, Pallas kernels, products(): pl.pallas_call(functools.partial(products_kernel, first, terms, CHI_DEV),...  44.2 us

commit v1 on v0

--- a/solution.py
+++ b/solution.py
@@ -328,6 +328,393 @@
     )(weights, dense.reshape((nz, ny) + dense.shape[1:]))
 
 
+def far_first(nz, z, k):
+    flip = z // (nz // 2)
+    m = z + flip * (nz - 1 - 2 * z)
+    ends = nz - 1 - k
+    inner = (1 - k % 2) * (nz - 1 - k // 2) + (k % 2) * (k // 2)
+    e = (1 - m) * ends + m * inner
+    return e + flip * (nz - 1 - 2 * e)
+
+
+def fused_kernel(nz, groups, terms, cap, weights, order, keep, slot, occ_idx, virt_idx, occ, virt,
+                 out, packed, y_out, y_in, z_right, z_left, lead_own, z2_right, z2_left, y2_in,
+                 times, y_send, y_recv, z_send, zr_recv, zl_recv, z2_send, z2r_recv, z2l_recv,
+                 y2_send, y2_recv, t_send, t_recv):
+    tau = lax.axis_index("tau")
+    tile = lax.axis_index("tile")
+    ny = 2
+    z, y = tile // ny, tile % ny
+    other_y = 1 - y
+    lead = lead_own.shape[0]
+    units = y_out.shape[1]
+    each, rows = y_out.shape[3], y_out.shape[4]
+    span = (units + lead) * each
+    owners = nz * ny
+    count = order.shape[0]
+    freqs = out.shape[0]
+
+    def dest(k):
+        return far_first(nz, z, k)
+
+    def remote(src, dst, send, recv, device):
+        return pltpu.make_async_remote_copy(
+            src_ref=src, dst_ref=dst, send_sem=send, recv_sem=recv,
+            device_id=device, device_id_type=MESH)
+
+    def y_copy(d, u):
+        k = d * units + u
+        return remote(y_out.at[d, u], y_in.at[d, u], y_send.at[k], y_recv.at[k],
+                      {"tile": z * ny + other_y})
+
+    def z_copy(right, d, u, src, back=False):
+        if right:
+            k = (d - 1) * units + u
+            dst, recv = z_right.at[d - 1, u], zr_recv.at[k]
+        else:
+            k = d * units + u
+            dst, recv = z_left.at[d, u], zl_recv.at[k]
+        return remote(src, dst, z_send.at[d * units + u], recv,
+                      {"tile": tile + (ny if right != back else -ny)})
+
+    def z2_copy(right, d, yy, w, src, back=False):
+        k = (d * ny + yy) * lead + w
+        if right:
+            dst, recv = z2_right.at[d - 1, yy, w], z2r_recv.at[k - ny * lead]
+        else:
+            dst, recv = z2_left.at[d, yy, w], z2l_recv.at[k]
+        return remote(src, dst, z2_send.at[k], recv,
+                      {"tile": tile + (ny if right != back else -ny)})
+
+    def y2_copy(w):
+        return remote(lead_own.at[w, z, other_y], y2_in.at[w], y2_send.at[w], y2_recv.at[w],
+                      {"tile": z * ny + other_y})
+
+    def swap(src, u, step):
+        other = (tau + step) % groups
+        return remote(src.at[other], times.at[u, tau], t_send.at[u * groups + step],
+                      t_recv.at[u * groups + tau], {"tau": other})
+
+    def arrived(u, source):
+        return remote(times.at[u, tau], times.at[u, source], t_send.at[u * groups],
+                      t_recv.at[u * groups + source], {"tau": source})
+
+    barrier = pltpu.get_barrier_semaphore()
+    for step in range(1, groups):
+        pl.semaphore_signal(barrier, inc=1, device_id={"tau": (tau + step) % groups},
+                            device_id_type=MESH)
+    pl.semaphore_signal(barrier, inc=1, device_id={"tile": z * ny + other_y}, device_id_type=MESH)
+    for step in range(1, nz):
+        pl.semaphore_signal(barrier, inc=1, device_id={"tile": (z + step) % nz * ny + y},
+                            device_id_type=MESH)
+    pl.semaphore_wait(barrier, groups - 1 + ny - 1 + nz - 1)
+
+    packed[0] = jnp.zeros(packed.shape[1:], packed.dtype)
+
+    def product(s):
+        p = order[s]
+        left = [occ[occ_idx[j, p]] for j in range(terms)]
+        right = [virt[virt_idx[j, p]] for j in range(terms)]
+        acc = jnp.dot(
+            jnp.concatenate(left, axis=1),
+            jnp.concatenate(right, axis=0),
+            preferred_element_type=jnp.float32,
+        )
+        packed[s + 1] = acc + keep[s] * packed[s]
+
+    def fill(rank, u, ref, add):
+        for e in range(each):
+            part = packed[slot[rank * span + u * each + e]]
+            for g in range(groups):
+                piece = part[g * rows:(g + 1) * rows]
+                if add:
+                    ref[g, e] += piece
+                else:
+                    ref[g, e] = piece
+
+    def ready(rank):
+        d = dest(rank // 2)
+        yy = y if rank % 2 else other_y
+        if rank % 2 == 0:
+            @pl.loop(0, units)
+            def _(u):
+                fill(rank, u, y_out.at[d, u], False)
+                y_copy(d, u).start()
+
+        @pl.loop(0, lead)
+        def _(w):
+            own = lead_own.at[w, d, yy]
+            fill(rank, units + w, own, False)
+
+            @pl.when((z == 0) & (d > z))
+            def _():
+                z2_copy(True, d, yy, w, own).start()
+
+            @pl.when((z == nz - 1) & (d < z))
+            def _():
+                z2_copy(False, d, yy, w, own).start()
+
+    def y_stage(i):
+        k, u = i // units, i % units
+        d = dest(k)
+        here = y_in.at[d, u]
+        y_copy(d, u).wait_recv()
+        fill(2 * k + 1, u, here, True)
+
+        @pl.when((z == 0) & (d > z))
+        def _():
+            z_copy(True, d, u, here).start()
+
+        @pl.when((z == nz - 1) & (d < z))
+        def _():
+            z_copy(False, d, u, here).start()
+
+    def z_stage(i):
+        k, u = i // units, i % units
+        d = dest(k)
+        own = y_in.at[d, u]
+
+        @pl.when((z > 0) & (d > z))
+        def _():
+            here = z_right.at[d - 1, u]
+            copy = z_copy(True, d, u, here)
+            copy.wait_recv()
+            here[...] += own[...]
+            copy.start()
+
+        @pl.when((z < nz - 1) & (d < z))
+        def _():
+            here = z_left.at[d, u]
+            copy = z_copy(False, d, u, here)
+            copy.wait_recv()
+            here[...] += own[...]
+            copy.start()
+
+        @pl.when((d == z) & (z > 0))
+        def _():
+            here = z_right.at[z - 1, u]
+            z_copy(True, z, u, here, True).wait_recv()
+            own[...] += here[...]
+
+        @pl.when((d == z) & (z < nz - 1))
+        def _():
+            here = z_left.at[z, u]
+            z_copy(False, z, u, here, True).wait_recv()
+            own[...] += here[...]
+
+        @pl.when(d == z)
+        def _():
+            for step in range(1, groups):
+                swap(own, u, step).start()
+            times[u, tau] = own[tau]
+
+    def lead_stage(j):
+        rank, w = j // lead, j % lead
+        d = dest(rank // 2)
+        yy = y + (1 - rank % 2) * (1 - 2 * y)
+        own = lead_own.at[w, d, yy]
+
+        @pl.when((z > 0) & (d > z))
+        def _():
+            here = z2_right.at[d - 1, yy, w]
+            copy = z2_copy(True, d, yy, w, here)
+            copy.wait_recv()
+            here[...] += own[...]
+            copy.start()
+
+        @pl.when((z < nz - 1) & (d < z))
+        def _():
+            here = z2_left.at[d, yy, w]
+            copy = z2_copy(False, d, yy, w, here)
+            copy.wait_recv()
+            here[...] += own[...]
+            copy.start()
+
+        @pl.when((d == z) & (z > 0))
+        def _():
+            here = z2_right.at[z - 1, yy, w]
+            z2_copy(True, z, yy, w, here, True).wait_recv()
+            own[...] += here[...]
+
+        @pl.when((d == z) & (z < nz - 1))
+        def _():
+            here = z2_left.at[z, yy, w]
+            z2_copy(False, z, yy, w, here, True).wait_recv()
+            own[...] += here[...]
+
+        @pl.when((d == z) & (rank % 2 == 0))
+        def _():
+            y2_copy(w).start()
+
+    def cross_stage(w):
+        own = lead_own.at[w, z, y]
+        y2_copy(w).wait_recv()
+        own[...] += y2_in[w]
+        for step in range(1, groups):
+            swap(own, units + w, step).start()
+        times[units + w, tau] = own[tau]
+
+    def out_stage(u):
+        for step in range(1, groups):
+            arrived(u, (tau + step) % groups).wait_recv()
+        for e in range(each):
+            for k in range(freqs):
+                total = weights[k, 0] * times[u, 0, e]
+                for s in range(1, groups):
+                    total += weights[k, s] * times[u, s, e]
+                out[k, u * each + e] = total
+
+    early = 0
+    phases = -(-count // cap)
+    for phase in range(phases):
+        @pl.loop(phase * cap, min(count, (phase + 1) * cap), unroll=2)
+        def _(s):
+            product(s)
+
+        for rank in range(phase, phase + 1 if phase < phases - 1 else owners):
+            ready(rank)
+        upto = early
+        if 1 <= phase < phases - 1:
+            upto = early + 2 * phase
+
+            @pl.loop(early, upto)
+            def _(i):
+                y_stage(i)
+        early = upto
+
+    items = nz * units
+    hold = 2
+    own_first = items - units + early
+
+    @pl.loop(early, items + early + lead + hold)
+    def _(t):
+        @pl.when(t < items)
+        def _():
+            y_stage(t)
+
+        @pl.when(t - early < owners * lead)
+        def _():
+            lead_stage(t - early)
+
+        @pl.when(t - early < items)
+        def _():
+            z_stage(t - early)
+
+        @pl.when((t >= items + early) & (t < items + early + lead))
+        def _():
+            cross_stage(t - items - early)
+
+        @pl.when(t >= own_first + hold)
+        def _():
+            out_stage(t - own_first - hold)
+
+    @pl.loop(0, units)
+    def _(u):
+        @pl.loop(0, nz)
+        def _(d):
+            y_copy(d, u).wait_send()
+
+            @pl.when(d > z)
+            def _():
+                z_copy(True, d, u, y_in.at[d, u]).wait_send()
+
+            @pl.when(d < z)
+            def _():
+                z_copy(False, d, u, y_in.at[d, u]).wait_send()
+
+        for step in range(1, groups):
+            swap(y_in.at[z, u], u, step).wait_send()
+
+    @pl.loop(0, lead)
+    def _(w):
+        @pl.loop(0, nz)
+        def _(d):
+            for yy in range(ny):
+                @pl.when(d > z)
+                def _():
+                    z2_copy(True, d, yy, w, lead_own.at[w, d, yy]).wait_send()
+
+                @pl.when(d < z)
+                def _():
+                    z2_copy(False, d, yy, w, lead_own.at[w, d, yy]).wait_send()
+
+        y2_copy(w).wait_send()
+        for step in range(1, groups):
+            swap(lead_own.at[w, z, y], units + w, step).wait_send()
+
+
+def slot_tables(target, nz, span):
+    ny = 2
+    tile = lax.axis_index("tile")
+    z, y = tile // ny, tile % ny
+    owner = target // span
+    zd, yd = owner // ny, owner % ny
+    rank = (yd == y).astype(jnp.int32)
+    for k in range(nz):
+        rank += jnp.where(zd == far_first(nz, z, k), 2 * k, 0)
+    key = rank * span + target % span
+    p = jnp.arange(key.shape[0], dtype=jnp.int32)
+    before = (key[None, :] < key[:, None]) | ((key[None, :] == key[:, None]) & (p[None, :] < p[:, None]))
+    position = jnp.sum(before.astype(jnp.int32), axis=1)
+    hit = position[None, :] == p[:, None]
+    order = jnp.sum(jnp.where(hit, p[None, :], 0), axis=1)
+    first = ~jnp.any((key[None, :] == key[:, None]) & (p[None, :] < p[:, None]), axis=1)
+    keep = jnp.sum(jnp.where(hit & ~first[None, :], 1.0, 0.0), axis=1)
+    place = jnp.arange(nz * ny * span, dtype=jnp.int32)
+    upto = jnp.sum((key[None, :] <= place[:, None]).astype(jnp.int32), axis=1)
+    named = jnp.any(key[None, :] == place[:, None], axis=1)
+    return order, keep, jnp.where(named, upto, 0)
+
+
+def fused(occ, virt, weights, occ_idx, virt_idx, target, nz, groups):
+    count, terms = occ_idx.shape
+    size = occ.shape[1]
+    ny, span = 2, CHI_DEV
+    each = UNIT
+    lead = max(1, int(span // each * Z_FIRST))
+    units = span // each - lead
+    rows = size // groups
+    block = (groups, each, rows, size)
+    freqs = weights.shape[0]
+    order, keep, slot = slot_tables(target, nz, span)
+    smem = pl.BlockSpec(memory_space=pltpu.SMEM)
+    vmem = pl.BlockSpec(memory_space=pltpu.VMEM)
+    dma = pltpu.SemaphoreType.DMA
+    f32 = jnp.float32
+    return pl.pallas_call(
+        functools.partial(fused_kernel, nz, groups, terms, 2 * count // (nz * ny)),
+        out_shape=jax.ShapeDtypeStruct((freqs, span, rows, size), f32),
+        in_specs=[smem] * 6 + [vmem] * 2,
+        out_specs=vmem,
+        scratch_shapes=[
+            pltpu.VMEM((count + 1, size, size), f32),
+            pltpu.VMEM((nz, units) + block, f32),
+            pltpu.VMEM((nz, units) + block, f32),
+            pltpu.VMEM((nz - 1, units) + block, f32),
+            pltpu.VMEM((nz - 1, units) + block, f32),
+            pltpu.VMEM((lead, nz, ny) + block, f32),
+            pltpu.VMEM((nz - 1, ny, lead) + block, f32),
+            pltpu.VMEM((nz - 1, ny, lead) + block, f32),
+            pltpu.VMEM((lead,) + block, f32),
+            pltpu.VMEM((units + lead,) + block, f32),
+            dma((nz * units,)),
+            dma((nz * units,)),
+            dma((nz * units,)),
+            dma(((nz - 1) * units,)),
+            dma(((nz - 1) * units,)),
+            dma((nz * ny * lead,)),
+            dma(((nz - 1) * ny * lead,)),
+            dma(((nz - 1) * ny * lead,)),
+            dma((lead,)),
+            dma((lead,)),
+            dma(((units + lead) * groups,)),
+            dma(((units + lead) * groups,)),
+        ],
+        compiler_params=pltpu.CompilerParams(
+            collective_id=0, has_side_effects=True, vmem_limit_bytes=62 * 1024 * 1024),
+    )(weights, order, keep, slot, occ_idx.T, virt_idx.T, occ, virt)
+
+
 def body(occupied, virtual, cos_weights, pair_occ, pair_virt, partial_target_tile):
     owners = lax.axis_size("tile")
     groups = lax.axis_size("tau")
@@ -336,6 +723,9 @@
     while 2 * ny * 2 * ny <= owners:
         ny *= 2
     nz = owners // ny
+    if ny == 2 and nz == 4:
+        return fused(occupied[0], virtual[0], cos_weights, pair_occ, pair_virt,
+                     partial_target_tile, nz, groups)
     tile_bytes = 4 * size * size
     span = CHI_DEV
     while span > UNIT and span * tile_bytes * (

time: 258 us -> 201 us (0.78); the launches traced: 254 us -> 201 us
  Pallas kernels: 251 us -> 195 us
  other arithmetic: 0 us -> 3.3 us
    pallas_call x2 -> x1, Pallas kernels: 251 us -> 195 us  [fused(): pl.pallas_call(functools.partial(fused_kernel, nz, groups, terms, 2 * cou...]
where the time goes in v1:
time: 201 us
  Pallas kernels  195 us (97%)
  other arithmetic  3.3 us (2%)
  local copies, waits for them, and re-layouts  3.08 us (2%)
    pallas_call x1, Pallas kernels, fused(): pl.pallas_call(functools.partial(fused_kernel, nz, groups, terms, 2 * cou...  195 us

profile of v1, /device:TPU:9, one launch (start us, length us, event | category | flops | bytes accessed | tf_op | source)
XLA Modules:
  0.0 200.9 jit_solution(1373086254976326541)
XLA Ops:
  0.0 0.7 fusion.8
  0.7 0.1 fusion.2
  0.8 0.2 fusion.3
  1.0 0.2 convert_reduce_fusion.1
  1.2 0.1 convert_reduce_fusion
  1.3 0.6 broadcast_select_fusion.slot
  1.9 0.7 select_reduce_fusion.keep
  2.6 0.7 select_reduce_fusion.1.order
  3.3 194.5 %shard_map.64 = f32[4,32,32,128]{3,2,1,0:T(8,128)} custom-call(f32[4,4]{1,0:T(4,128)} %weights.1, s32[192]{0:T(256)} %select_reduce_fusion.1.order, f32[192]{0:T(256)} %select_reduce_fusion.keep, s32[256]{0:T(256)} %broadcast_select_fusion.slot, s32[16,192]{1,0:T(8,128)} %bitcast.6, s32[16,192]{1,0:T(8,128)} %bitcast.7, bf16[128,128,128]{2,1,0:T(8,128)(2,1)} %bitcast.4, ...), custom_call_target="tpu_custom_call" | custom-call | tf_op jit(solution)/shard_map/pallas_call | solution.py:684
  197.8 3.1 %copy.8 = f32[4,32,32,128]{3,2,1,0:T(8,128)} copy(f32[4,32,32,128]{3,2,1,0:T(8,128)} %shard_map.64) | data formatting | bytes 4194304

commit v2 on v1

--- a/solution.py
+++ b/solution.py
@@ -337,8 +337,8 @@
     return e + flip * (nz - 1 - 2 * e)
 
 
-def fused_kernel(nz, groups, terms, cap, weights, order, keep, slot, occ_idx, virt_idx, occ, virt,
-                 out, packed, y_out, y_in, z_right, z_left, lead_own, z2_right, z2_left, y2_in,
+def fused_kernel(nz, groups, terms, cap, weights, order, slot, occ_idx, virt_idx, occ_hbm, virt_hbm,
+                 out, occ, virt, load_sem, packed, y_out, y_in, z_right, z_left, lead_own, z2_right, z2_left, y2_in,
                  times, y_send, y_recv, z_send, zr_recv, zl_recv, z2_send, z2r_recv, z2l_recv,
                  y2_send, y2_recv, t_send, t_recv):
     tau = lax.axis_index("tau")
@@ -399,6 +399,11 @@
         return remote(times.at[u, tau], times.at[u, source], t_send.at[u * groups],
                       t_recv.at[u * groups + source], {"tau": source})
 
+    loads = [pltpu.make_async_copy(occ_hbm, occ, load_sem.at[0]),
+             pltpu.make_async_copy(virt_hbm, virt, load_sem.at[1])]
+    for load in loads:
+        load.start()
+
     barrier = pltpu.get_barrier_semaphore()
     for step in range(1, groups):
         pl.semaphore_signal(barrier, inc=1, device_id={"tau": (tau + step) % groups},
@@ -410,9 +415,12 @@
     pl.semaphore_wait(barrier, groups - 1 + ny - 1 + nz - 1)
 
     packed[0] = jnp.zeros(packed.shape[1:], packed.dtype)
+    for load in loads:
+        load.wait()
 
     def product(s):
-        p = order[s]
+        p = order[s] // 2
+        keep = (order[s] % 2).astype(jnp.float32)
         left = [occ[occ_idx[j, p]] for j in range(terms)]
         right = [virt[virt_idx[j, p]] for j in range(terms)]
         acc = jnp.dot(
@@ -420,7 +428,7 @@
             jnp.concatenate(right, axis=0),
             preferred_element_type=jnp.float32,
         )
-        packed[s + 1] = acc + keep[s] * packed[s]
+        packed[s + 1] = acc + keep * packed[s]
 
     def fill(rank, u, ref, add):
         for e in range(each):
@@ -439,7 +447,8 @@
             @pl.loop(0, units)
             def _(u):
                 fill(rank, u, y_out.at[d, u], False)
-                y_copy(d, u).start()
+                if rank < owners - ny:
+                    y_copy(d, u).start()
 
         @pl.loop(0, lead)
         def _(w):
@@ -567,7 +576,7 @@
     early = 0
     phases = -(-count // cap)
     for phase in range(phases):
-        @pl.loop(phase * cap, min(count, (phase + 1) * cap), unroll=2)
+        @pl.loop(phase * cap, min(count, (phase + 1) * cap), unroll=8)
         def _(s):
             product(s)
 
@@ -583,30 +592,45 @@
         early = upto
 
     items = nz * units
-    hold = 2
-    own_first = items - units + early
-
-    @pl.loop(early, items + early + lead + hold)
+    passing = items - units
+    hold, lag = 2, 3
+    last = early + owners * lead
+
+    @pl.loop(early, items + lag + hold)
     def _(t):
         @pl.when(t < items)
         def _():
             y_stage(t)
 
-        @pl.when(t - early < owners * lead)
+        @pl.when(t < last)
         def _():
             lead_stage(t - early)
 
-        @pl.when(t - early < items)
+        @pl.when(t == last)
+        def _():
+            @pl.loop(0, units)
+            def _(u):
+                y_copy(z, u).start()
+
+        @pl.when(t < passing + early)
         def _():
             z_stage(t - early)
 
-        @pl.when((t >= items + early) & (t < items + early + lead))
-        def _():
-            cross_stage(t - items - early)
-
-        @pl.when(t >= own_first + hold)
-        def _():
-            out_stage(t - own_first - hold)
+        @pl.when((t >= passing + lag) & (t < items + lag))
+        def _():
+            z_stage(t - lag)
+
+        @pl.when((t >= passing + early) & (t < passing + early + lead))
+        def _():
+            cross_stage(t - passing - early)
+
+        @pl.when((t >= passing + early + hold) & (t < passing + early + hold + lead))
+        def _():
+            out_stage(t - passing - early - hold + units)
+
+        @pl.when(t >= passing + lag + hold)
+        def _():
+            out_stage(t - passing - lag - hold)
 
     @pl.loop(0, units)
     def _(u):
@@ -656,14 +680,14 @@
     p = jnp.arange(key.shape[0], dtype=jnp.int32)
     before = (key[None, :] < key[:, None]) | ((key[None, :] == key[:, None]) & (p[None, :] < p[:, None]))
     position = jnp.sum(before.astype(jnp.int32), axis=1)
-    hit = position[None, :] == p[:, None]
-    order = jnp.sum(jnp.where(hit, p[None, :], 0), axis=1)
-    first = ~jnp.any((key[None, :] == key[:, None]) & (p[None, :] < p[:, None]), axis=1)
-    keep = jnp.sum(jnp.where(hit & ~first[None, :], 1.0, 0.0), axis=1)
+    again = jnp.any((key[None, :] == key[:, None]) & (p[None, :] < p[:, None]), axis=1)
+    code = 2 * p + again.astype(jnp.int32)
+    order = jnp.sum(jnp.where(position[None, :] == p[:, None], code[None, :], 0), axis=1)
     place = jnp.arange(nz * ny * span, dtype=jnp.int32)
-    upto = jnp.sum((key[None, :] <= place[:, None]).astype(jnp.int32), axis=1)
-    named = jnp.any(key[None, :] == place[:, None], axis=1)
-    return order, keep, jnp.where(named, upto, 0)
+    big = 2 * key.shape[0]
+    found = jnp.sum((key[None, :] <= place[:, None]).astype(jnp.int32)
+                    + jnp.where(key[None, :] == place[:, None], big, 0), axis=1)
+    return order, jnp.where(found >= big, found % big, 0)
 
 
 def fused(occ, virt, weights, occ_idx, virt_idx, target, nz, groups):
@@ -676,7 +700,7 @@
     rows = size // groups
     block = (groups, each, rows, size)
     freqs = weights.shape[0]
-    order, keep, slot = slot_tables(target, nz, span)
+    order, slot = slot_tables(target, nz, span)
     smem = pl.BlockSpec(memory_space=pltpu.SMEM)
     vmem = pl.BlockSpec(memory_space=pltpu.VMEM)
     dma = pltpu.SemaphoreType.DMA
@@ -684,9 +708,12 @@
     return pl.pallas_call(
         functools.partial(fused_kernel, nz, groups, terms, 2 * count // (nz * ny)),
         out_shape=jax.ShapeDtypeStruct((freqs, span, rows, size), f32),
-        in_specs=[smem] * 6 + [vmem] * 2,
+        in_specs=[smem] * 5 + [pl.BlockSpec(memory_space=pl.ANY)] * 2,
         out_specs=vmem,
         scratch_shapes=[
+            pltpu.VMEM(occ.shape, occ.dtype),
+            pltpu.VMEM(virt.shape, virt.dtype),
+            dma((2,)),
             pltpu.VMEM((count + 1, size, size), f32),
             pltpu.VMEM((nz, units) + block, f32),
             pltpu.VMEM((nz, units) + block, f32),
@@ -712,7 +739,7 @@
         ],
         compiler_params=pltpu.CompilerParams(
             collective_id=0, has_side_effects=True, vmem_limit_bytes=62 * 1024 * 1024),
-    )(weights, order, keep, slot, occ_idx.T, virt_idx.T, occ, virt)
+    )(weights, order, slot, occ_idx.T, virt_idx.T, occ, virt)
 
 
 def body(occupied, virtual, cos_weights, pair_occ, pair_virt, partial_target_tile):

time: 201 us -> 191 us (0.950)
  Pallas kernels: 195 us -> 184 us
    pallas_call x1, Pallas kernels: 195 us -> 184 us  [fused(): pl.pallas_call(functools.partial(fused_kernel, nz, groups, terms, 2 * cou...]
where the time goes in v2:
time: 191 us; the launch traced here: 189 us
  Pallas kernels  184 us (96%)
  local copies, waits for them, and re-layouts  3.08 us (2%)
  other arithmetic  2.5 us (1%)
    pallas_call x1, Pallas kernels, fused(): pl.pallas_call(functools.partial(fused_kernel, nz, groups, terms, 2 * cou...  184 us

profile of v2, /device:TPU:9, one launch (start us, length us, event | category | flops | bytes accessed | tf_op | source)
XLA Modules:
  0.0 189.3 jit_solution(18385993744870182201)
XLA Ops:
  0.0 0.7 fusion.6
  0.7 0.2 fusion.1
  0.9 0.1 add_reduce_fusion
  1.0 0.2 convert_reduce_fusion
  1.2 0.7 select_reduce_fusion.order
  1.9 0.6 compare_select_fusion.slot
  2.5 183.7 %shard_map.64 = f32[4,32,32,128]{3,2,1,0:T(8,128)} custom-call(f32[4,4]{1,0:T(4,128)} %weights.1, s32[192]{0:T(256)} %select_reduce_fusion.order, s32[256]{0:T(256)} %compare_select_fusion.slot, s32[16,192]{1,0:T(8,128)} %bitcast.6, s32[16,192]{1,0:T(8,128)} %bitcast.7, bf16[128,128,128]{2,1,0:T(8,128)(2,1)} %bitcast.4, bf16[128,128,128]{2,1,0:T(8,128)(2,1)} %bitcast.5), custom_call_target="tpu_custom_call" | custom-call | tf_op jit(solution)/shard_map/pallas_call | solution.py:708
  186.2 3.1 %copy.8 = f32[4,32,32,128]{3,2,1,0:T(8,128)} copy(f32[4,32,32,128]{3,2,1,0:T(8,128)} %shard_map.64) | data formatting | bytes 4194304
  (1 shorter events, 0.0 us)

commit v3 on v2

--- a/solution.py
+++ b/solution.py
@@ -409,10 +409,16 @@
         pl.semaphore_signal(barrier, inc=1, device_id={"tau": (tau + step) % groups},
                             device_id_type=MESH)
     pl.semaphore_signal(barrier, inc=1, device_id={"tile": z * ny + other_y}, device_id_type=MESH)
-    for step in range(1, nz):
-        pl.semaphore_signal(barrier, inc=1, device_id={"tile": (z + step) % nz * ny + y},
-                            device_id_type=MESH)
-    pl.semaphore_wait(barrier, groups - 1 + ny - 1 + nz - 1)
+    @pl.when(z > 0)
+    def _():
+        pl.semaphore_signal(barrier, inc=1, device_id={"tile": tile - ny}, device_id_type=MESH)
+
+    @pl.when(z < nz - 1)
+    def _():
+        pl.semaphore_signal(barrier, inc=1, device_id={"tile": tile + ny}, device_id_type=MESH)
+
+    beside = (z + nz - 1) // nz + (2 * nz - 2 - z) // nz
+    pl.semaphore_wait(barrier, groups - 1 + ny - 1 + beside)
 
     packed[0] = jnp.zeros(packed.shape[1:], packed.dtype)
     for load in loads:
@@ -576,7 +582,7 @@
     early = 0
     phases = -(-count // cap)
     for phase in range(phases):
-        @pl.loop(phase * cap, min(count, (phase + 1) * cap), unroll=8)
+        @pl.loop(phase * cap, min(count, (phase + 1) * cap), unroll=16)
         def _(s):
             product(s)
 
@@ -707,7 +713,7 @@
     f32 = jnp.float32
     return pl.pallas_call(
         functools.partial(fused_kernel, nz, groups, terms, 2 * count // (nz * ny)),
-        out_shape=jax.ShapeDtypeStruct((freqs, span, rows, size), f32),
+        out_shape=pltpu.VMEM((freqs, span, rows, size), f32),
         in_specs=[smem] * 5 + [pl.BlockSpec(memory_space=pl.ANY)] * 2,
         out_specs=vmem,
         scratch_shapes=[
@@ -738,7 +744,7 @@
             dma(((units + lead) * groups,)),
         ],
         compiler_params=pltpu.CompilerParams(
-            collective_id=0, has_side_effects=True, vmem_limit_bytes=62 * 1024 * 1024),
+            collective_id=0, has_side_effects=True, vmem_limit_bytes=57 * 1024 * 1024),
     )(weights, order, slot, occ_idx.T, virt_idx.T, occ, virt)
 
 

time: 191 us -> 187 us (0.979)
  Pallas kernels: 184 us -> 182 us
where the time goes in v3:
time: 187 us; the launch traced here: 186 us
  Pallas kernels  182 us (97%)
  other arithmetic  2.5 us (1%)
    pallas_call x1, Pallas kernels, fused(): pl.pallas_call(functools.partial(fused_kernel, nz, groups, terms, 2 * cou...  182 us

profile of v3, /device:TPU:9, one launch (start us, length us, event | category | flops | bytes accessed | tf_op | source)
XLA Modules:
  0.0 185.7 jit_solution(16303355845317588795)
XLA Ops:
  0.0 0.7 fusion.6
  0.7 0.2 fusion.1
  0.9 0.1 add_reduce_fusion
  1.0 0.2 convert_reduce_fusion
  1.2 0.7 select_reduce_fusion.order
  1.9 0.6 compare_select_fusion.slot
  2.5 181.9 %shard_map.64 = f32[4,32,32,128]{3,2,1,0:T(8,128)S(1)} custom-call(f32[4,4]{1,0:T(4,128)} %weights.1, s32[192]{0:T(256)} %select_reduce_fusion.order, s32[256]{0:T(256)} %compare_select_fusion.slot, s32[16,192]{1,0:T(8,128)} %bitcast.6, s32[16,192]{1,0:T(8,128)} %bitcast.7, bf16[128,128,128]{2,1,0:T(8,128)(2,1)} %bitcast.4, bf16[128,128,128]{2,1,0:T(8,128)(2,1)} %bitcast.5), custom_call_target="tpu_custom_call" | custom-call | tf_op jit(solution)/shard_map/pallas_call | solution.py:714
  184.4 1.3 copy.8
  (1 shorter events, 0.0 us)

commit v4 on v3

--- a/solution.py
+++ b/solution.py
@@ -449,6 +449,19 @@
     def ready(rank):
         d = dest(rank // 2)
         yy = y if rank % 2 else other_y
+        @pl.loop(0, lead)
+        def _(w):
+            own = lead_own.at[w, d, yy]
+            fill(rank, units + w, own, False)
+
+            @pl.when((z == 0) & (d > z))
+            def _():
+                z2_copy(True, d, yy, w, own).start()
+
+            @pl.when((z == nz - 1) & (d < z))
+            def _():
+                z2_copy(False, d, yy, w, own).start()
+
         if rank % 2 == 0:
             @pl.loop(0, units)
             def _(u):
@@ -456,19 +469,6 @@
                 if rank < owners - ny:
                     y_copy(d, u).start()
 
-        @pl.loop(0, lead)
-        def _(w):
-            own = lead_own.at[w, d, yy]
-            fill(rank, units + w, own, False)
-
-            @pl.when((z == 0) & (d > z))
-            def _():
-                z2_copy(True, d, yy, w, own).start()
-
-            @pl.when((z == nz - 1) & (d < z))
-            def _():
-                z2_copy(False, d, yy, w, own).start()
-
     def y_stage(i):
         k, u = i // units, i % units
         d = dest(k)
@@ -483,6 +483,15 @@
         @pl.when((z == nz - 1) & (d < z))
         def _():
             z_copy(False, d, u, here).start()
+
+    def z_sent(d, u):
+        @pl.when(d > z)
+        def _():
+            z_copy(True, d, u, y_in.at[d, u]).wait_send()
+
+        @pl.when(d < z)
+        def _():
+            z_copy(False, d, u, y_in.at[d, u]).wait_send()
 
     def z_stage(i):
         k, u = i // units, i % units
@@ -638,20 +647,18 @@
         def _():
             out_stage(t - passing - lag - hold)
 
+        @pl.when((t >= passing + lag) & (t < items + lag))
+        def _():
+            u = t - passing - lag
+            for k in range(nz - 1):
+                y_copy(dest(k), u).wait_send()
+            for k in range(nz - 2):
+                z_sent(dest(k), u)
+
     @pl.loop(0, units)
     def _(u):
-        @pl.loop(0, nz)
-        def _(d):
-            y_copy(d, u).wait_send()
-
-            @pl.when(d > z)
-            def _():
-                z_copy(True, d, u, y_in.at[d, u]).wait_send()
-
-            @pl.when(d < z)
-            def _():
-                z_copy(False, d, u, y_in.at[d, u]).wait_send()
-
+        y_copy(z, u).wait_send()
+        z_sent(dest(nz - 2), u)
         for step in range(1, groups):
             swap(y_in.at[z, u], u, step).wait_send()
 

time: 187 us -> 186 us (level)
  no operation moved by 1% of the time
where the time goes in v4:
time: 186 us; the launch traced here: 185 us
  Pallas kernels  181 us (97%)
  other arithmetic  2.5 us (1%)
    pallas_call x1, Pallas kernels, fused(): pl.pallas_call(functools.partial(fused_kernel, nz, groups, terms, 2 * cou...  181 us

profile of v4, /device:TPU:9, one launch (start us, length us, event | category | flops | bytes accessed | tf_op | source)
XLA Modules:
  0.0 185.0 jit_solution(9837363060459168739)
XLA Ops:
  0.0 0.7 fusion.6
  0.7 0.2 fusion.1
  0.9 0.1 add_reduce_fusion
  1.0 0.2 convert_reduce_fusion
  1.2 0.7 select_reduce_fusion.order
  1.9 0.6 compare_select_fusion.slot
  2.5 181.2 %shard_map.64 = f32[4,32,32,128]{3,2,1,0:T(8,128)S(1)} custom-call(f32[4,4]{1,0:T(4,128)} %weights.1, s32[192]{0:T(256)} %select_reduce_fusion.order, s32[256]{0:T(256)} %compare_select_fusion.slot, s32[16,192]{1,0:T(8,128)} %bitcast.6, s32[16,192]{1,0:T(8,128)} %bitcast.7, bf16[128,128,128]{2,1,0:T(8,128)(2,1)} %bitcast.4, bf16[128,128,128]{2,1,0:T(8,128)(2,1)} %bitcast.5), custom_call_target="tpu_custom_call" | custom-call | tf_op jit(solution)/shard_map/pallas_call | solution.py:721
  183.7 1.3 copy.8
  (1 shorter events, 0.0 us)
